TPU v7x, 32 devices: a whole 2x2x4 slice. The times are simulated.
32 devices in a mesh: dp: 2 (over x), tp: 4 (over z), section: 4 (over y, core).
Axes of the slice: x: 2, y: 2, z: 4, core: 2. Of those that a mesh axis runs over, the one named last changes fastest.
Arguments:
- tokens: bfloat16 [256, 2304], P('dp', 'section'), may hold values from -6 to 6
- hidden_grad: bfloat16 [256, 18432], P('dp', ('tp', 'section')), may hold values from -6 to 6
- norm_gain: float32 [2304], replicated, may hold values from 0.5 to 1.5
- w_gate: bfloat16 [2304, 18432], P('dp', ('tp', 'section')), may hold values from -0.125 to 0.125
- w_up: bfloat16 [2304, 18432], P('dp', ('tp', 'section')), may hold values from -0.125 to 0.125
Outputs:
- grad_tokens: bfloat16 [256, 2304], P('dp', ('tp', 'section'))
- grad_gain: float32 [2304], P(('tp', 'section'))
- grad_gate: bfloat16 [2304, 18432], P('dp', ('tp', 'section'))
- grad_up: bfloat16 [2304, 18432], P('dp', ('tp', 'section'))
All inputs are finite; a program needn't handle non-finite values.
Results may differ from a plain program's by a relative error of at most 0.018.
Values may be sent and summed in bfloat16 or wider, within the bound.
A program may use at most 128 MiB of HBM per device.

v0:
```python
import jax
import jax.numpy as jnp
from jax import lax
from jax.sharding import PartitionSpec as P

D = 2304
epsilon = 1e-06


def gated_unit(gate, up):
    return jax.nn.gelu(gate, approximate=True) * up


def shards(tokens, hidden_grad, norm_gain, w_gate, w_up):
    rows_in = lax.all_gather(tokens, "section", axis=1, tiled=True)
    inputs = rows_in.astype(jnp.float32)
    inv_rms = lax.rsqrt(jnp.mean(inputs * inputs, axis=1) + epsilon)
    normed = (inputs * inv_rms[:, None] * norm_gain).astype(jnp.bfloat16)
    full_gate, full_up = (
        lax.all_gather(w_gate, "dp", axis=0, tiled=True),
        lax.all_gather(w_up, "dp", axis=0, tiled=True),
    )
    gate = jnp.dot(normed, full_gate, preferred_element_type=jnp.float32)
    up = jnp.dot(normed, full_up, preferred_element_type=jnp.float32)
    hidden, pull = jax.vjp(gated_unit, gate, up)
    d_gate, d_up = pull(hidden_grad.astype(jnp.float32))
    d_gate = d_gate.astype(jnp.bfloat16)
    d_up = d_up.astype(jnp.bfloat16)
    contract_cols = (((1,), (1,)), ((), ()))
    contract_rows = (((0,), (0,)), ((), ()))
    features = full_gate.shape[0]
    own_width = features // lax.axis_size(("tp", "section"))
    first = lax.dot_general(full_gate, d_gate, contract_cols, preferred_element_type=jnp.float32)
    second = lax.dot_general(full_up, d_up, contract_cols, preferred_element_type=jnp.float32)
    d_columns = lax.psum_scatter(
        (first + second).astype(jnp.bfloat16), ("tp", "section"), scatter_dimension=0, tiled=True
    ).astype(jnp.float32)
    d_normed = d_columns.T
    offset = lax.axis_index(("tp", "section")) * own_width
    own_inputs = lax.dynamic_slice_in_dim(inputs, offset, own_width, 1)
    own_gain = lax.dynamic_slice_in_dim(norm_gain, offset, own_width, 0)
    gain_part = jnp.sum(d_normed * own_inputs * inv_rms[:, None], axis=0)
    row_part = jnp.sum(own_inputs * own_gain * d_normed, axis=1)
    grad_gain = lax.psum(gain_part, "dp")
    row_sum = lax.psum(row_part, ("tp", "section"))
    grad_tokens = (
        inv_rms[:, None] * own_gain * d_normed - own_inputs * (inv_rms**3 * row_sum / D)[:, None]
    )
    block = w_gate.shape[0]
    fwidth = w_gate.shape[1]
    cols_normed = lax.all_to_all(normed, "dp", split_axis=1, concat_axis=0, tiled=True)
    per_device = normed.shape[0]
    empty = jnp.zeros((block, fwidth), jnp.float32)
    piece_gate = lax.all_gather(d_gate, "dp", axis=0, tiled=True)
    piece_up = lax.all_gather(d_up, "dp", axis=0, tiled=True)

    def one_block(index, running):
        inner = index * per_device
        block_normed = lax.dynamic_slice_in_dim(cols_normed, inner, per_device, 0)
        block_gate = lax.dynamic_slice_in_dim(piece_gate, inner, per_device, 0)
        block_up = lax.dynamic_slice_in_dim(piece_up, inner, per_device, 0)
        terms = (
            lax.dot_general(
                block_normed, block_gate, contract_rows, preferred_element_type=jnp.float32
            ),
            lax.dot_general(
                block_normed, block_up, contract_rows, preferred_element_type=jnp.float32
            ),
        )
        return tuple(
            (
                total + lax.optimization_barrier(term.astype(jnp.bfloat16)).astype(jnp.float32)
                for total, term in zip(running, terms)
            )
        )

    sum_gate, sum_up = lax.fori_loop(
        0, piece_gate.shape[0] // per_device, one_block, (empty, empty)
    )
    return (
        grad_tokens.astype(jnp.bfloat16),
        grad_gain,
        sum_gate.astype(jnp.bfloat16),
        sum_up.astype(jnp.bfloat16),
    )


def solution(mesh):
    in_specs = (
        P("dp", "section"),
        P("dp", ("tp", "section")),
        P(),
        P("dp", ("tp", "section")),
        P("dp", ("tp", "section")),
    )
    out_specs = (
        P("dp", ("tp", "section")),
        P(("tp", "section")),
        P("dp", ("tp", "section")),
        P("dp", ("tp", "section")),
    )
    return jax.shard_map(shards, mesh=mesh, in_specs=in_specs, out_specs=out_specs, check_vma=False)
```

profile of v0, /device:TPU:0, one launch (start us, length us, event | category | flops | bytes accessed | tf_op | source)
XLA Modules:
  0.0 266.3 jit_solution(6498756828406113752)
XLA Ops:
  8.7 9.0 %all_gather.15 = bf16[128,2304]{0,1:T(8,128)(2,1)S(1)} all-gather(bf16[128,576]{0,1:T(8,128)(2,1)S(1)} %copy-done.3), channel_id=1, replica_groups=mesh['dp'=2,'tp'=4,'section'=4] {'section'}, dimensions={1}, use_global_device_ids=true | all-gather | bytes 737280 | tf_op jit(solution)/shard_map/all_gather | solution.py:15
  19.5 3.5 %all-to-all-start = ((bf16[128,2,1152]{2,0,1:T(8,128)(2,1)}), bf16[128,2,1152]{2,0,1:T(8,128)(2,1)S(1)}, u32[]{:S(2)}, u32[]{:S(2)}) async-start(bf16[128,2,1152]{2,0,1:T(8,128)(2,1)} %copy.13), calls=%async_computation | async-start | bytes 1179648 | tf_op jit(solution)/shard_map/all_to_all | solution.py:51
  23.1 1.1 convert_element_type.59
  24.3 63.6 %all-gather.5.cloned.1.call-done = bf16[2304,1152]{1,0:T(8,128)(2,1)} async-done(((bf16[1152,1152]{1,0:T(8,128)(2,1)}), bf16[2304,1152]{1,0:T(8,128)(2,1)}) %all-gather.5.cloned.1.call-update) | async-done | bytes 5308432 | tf_op jit(solution)/shard_map/all_gather | solution.py:20
  87.9 3.7 %fusion.8 = (bf16[128,1152]{1,0:T(8,128)(2,1)S(1)}, f32[128,1152]{1,0:T(8,128)S(1)}) fusion(bf16[128,1152]{1,0:T(8,128)(2,1)S(1)} %copy-done.2, bf16[128,2304]{0,1:T(8,128)(2,1)S(1)} %multiply_convert_fusion, bf16[2304,1152]{1,0:T(8,128)(2,1)} %all-gather.5.cloned.1.call-done), kind=kOutput, calls=%fused_computation.19 | convolution fusion | flops 681099264 | bytes 7077888 | tf_op jit(solution)/shard_map/dot_general | solution.py:23
  91.6 67.1 %all-gather.3.cloned.1.call-done = bf16[2304,1152]{1,0:T(8,128)(2,1)} async-done(((bf16[1152,1152]{1,0:T(8,128)(2,1)}), bf16[2304,1152]{1,0:T(8,128)(2,1)}) %all-gather.3.cloned.1.call-update) | async-done | bytes 5308432 | tf_op jit(solution)/shard_map/all_gather | solution.py:21
  158.7 4.0 %fusion.15 = bf16[128,1152]{1,0:T(8,128)(2,1)S(1)} fusion(f32[128,1152]{1,0:T(8,128)S(1)} %get-tuple-element.158, bf16[128,2304]{0,1:T(8,128)(2,1)S(1)} %multiply_convert_fusion, bf16[2304,1152]{1,0:T(8,128)(2,1)} %all-gather.3.cloned.1.call-done, bf16[128,1152]{1,0:T(8,128)(2,1)} %param.8), kind=kOutput, calls=%fused_computation.26 | convolution fusion | flops 682721280 | bytes 7077888 | tf_op jit(solution)/shard_map/dot_general | solution.py:24
  162.7 1.6 fusion.23
  165.2 1.6 fusion.7
  167.9 9.3 %all_gather.19 = bf16[256,1152]{1,0:T(8,128)(2,1)} all-gather(bf16[128,1152]{1,0:T(8,128)(2,1)S(1)} %get-tuple-element.157), channel_id=1, replica_groups=mesh['dp'=2,'tp'=4,'section'=4] {'dp'}, dimensions={0}, use_global_device_ids=true | all-gather | bytes 884736 | tf_op jit(solution)/shard_map/all_gather | solution.py:55
  177.2 8.5 %all_gather.18 = bf16[256,1152]{1,0:T(8,128)(2,1)} all-gather(bf16[128,1152]{1,0:T(8,128)(2,1)S(1)} %fusion.15), channel_id=1, replica_groups=mesh['dp'=2,'tp'=4,'section'=4] {'dp'}, dimensions={0}, use_global_device_ids=true | all-gather | bytes 884736 | tf_op jit(solution)/shard_map/all_gather | solution.py:54
  185.7 27.0 %while.16 = (s32[]{:T(128)}, f32[1152,1152]{1,0:T(8,128)}, f32[1152,1152]{1,0:T(8,128)}, bf16[256,1152]{1,0:T(8,128)(2,1)S(1)}, bf16[256,1152]{1,0:T(8,128)(2,1)...) while((s32[]{:T(128)}, f32[1152,1152]{1,0:T(8,128)}, ...), condition=%wide.region_7.0_spmd.clone, body=%wide.region_6.0_spmd.clone.sunk | while | flops 690094080 | bytes 33032356 | solution.py:77
  185.7 1.8 convolution_convert_fusion.4
  187.6 3.4 %convolution_convert_fusion.5 = bf16[1152,1152]{1,0:T(8,128)(2,1)} fusion(bf16[256,1152]{1,0:T(8,128)(2,1)} %get-tuple-element.224, s32[]{:T(128)S(6)} %select_n.16, bf16[256,1152]{1,0:T(8,128)(2,1)S(1)} %get-tuple-element.223), kind=kOutput, calls=%fused_computation.1.clone.1 | convolution fusion | flops 341065728 | bytes 3245056 | tf_op jit(solution)/shard_map/while/body/eval_jaxpr/dot_general | solution.py:63
  190.9 6.7 %select_add_fusion.3 = (f32[1152,1152]{1,0:T(8,128)}, f32[1152,1152]{1,0:T(8,128)}) fusion(f32[1152,1152]{1,0:T(8,128)} %get-tuple-element.212, bf16[1152,1152]{1,0:T(8,128)(2,1)S(1)} %convolution_convert_fusion.4, pred[]{:T(512)S(6)} %compare.3, bf16[1152,1152]{1,0:T(8,128)(2,1)} %convolution_convert_fusion.5, f32[1152,1152]{1,0:T(8,128)} %get-tuple-element.211), kind=kLoop, calls=%fused_computation.2.clone.1 | loop fusion | flops 7962624 | bytes 26542080 | tf_op jit(solution)/shard_map/while/body/eval_jaxpr/add | solution.py:72
  197.6 1.8 convolution_convert_fusion.4
  199.5 3.4 %convolution_convert_fusion.5 = bf16[1152,1152]{1,0:T(8,128)(2,1)} fusion(bf16[256,1152]{1,0:T(8,128)(2,1)} %get-tuple-element.224, s32[]{:T(128)S(6)} %select_n.16, bf16[256,1152]{1,0:T(8,128)(2,1)S(1)} %get-tuple-element.223), kind=kOutput, calls=%fused_computation.1.clone.1 | convolution fusion | flops 341065728 | bytes 3245056 | tf_op jit(solution)/shard_map/while/body/eval_jaxpr/dot_general | solution.py:63
  202.8 9.9 %select_add_fusion.3 = (f32[1152,1152]{1,0:T(8,128)}, f32[1152,1152]{1,0:T(8,128)}) fusion(f32[1152,1152]{1,0:T(8,128)} %get-tuple-element.212, bf16[1152,1152]{1,0:T(8,128)(2,1)S(1)} %convolution_convert_fusion.4, pred[]{:T(512)S(6)} %compare.3, bf16[1152,1152]{1,0:T(8,128)(2,1)} %convolution_convert_fusion.5, f32[1152,1152]{1,0:T(8,128)} %get-tuple-element.211), kind=kLoop, calls=%fused_computation.2.clone.1 | loop fusion | flops 7962624 | bytes 26542080 | tf_op jit(solution)/shard_map/while/body/eval_jaxpr/add | solution.py:72
  212.7 4.4 %convert_element_type.68 = bf16[1152,1152]{1,0:T(8,128)(2,1)} convert(f32[1152,1152]{1,0:T(8,128)} %get-tuple-element.115) | non-fusion elementwise | flops 1327104 | bytes 7962624 | tf_op jit(solution)/shard_map/convert_element_type | solution.py:84
  217.3 1.8 convert_element_type.67
  219.1 3.0 %reduce-scatter.4.cloned.1.call-done = bf16[144,128]{1,0:T(8,128)(2,1)} async-done(((bf16[2304,128]{1,0:T(8,128)(2,1)}), bf16[144,128]{1,0:T(8,128)(2,1)}) %reduce-scatter.4.cloned.1.call-update) | async-done | bytes 36880 | tf_op jit(solution)/shard_map/reduce_scatter | solution.py:35
  223.2 5.5 %psum.15 = f32[144]{0:T(256)} all-reduce(f32[144]{0:T(256)S(1)} %get-tuple-element.141), channel_id=1, replica_groups=mesh['dp'=2,'tp'=4,'section'=4] {'dp'}, use_global_device_ids=true, to_apply=%region_5.0 | all-reduce | flops 144 | bytes 1152 | tf_op jit(solution)/shard_map/psum | solution.py:44
  228.6 29.5 %psum.14 = f32[128]{0:T(128)S(1)} all-reduce(f32[128]{0:T(128)S(1)} %get-tuple-element.142), channel_id=1, replica_groups=mesh['dp'=2,'tp'=4,'section'=4] {'tp','section'}, use_global_device_ids=true, to_apply=%region_3.0 | all-reduce | flops 128 | bytes 1024 | tf_op jit(solution)/shard_map/psum | solution.py:45
  258.1 1.6 fusion.17
  (32 shorter events, 6.7 us)
Async XLA Ops:
  7.2 1.5 copy-start.3
  7.2 10.9 %copy-start.4 = (f32[2304]{0:T(1024)S(1)}, f32[2304]{0:T(1024)}, u32[]{:S(2)}) copy-start(f32[2304]{0:T(1024)} %param.9) | copy-start | bytes 27652
  7.2 80.7 %all-gather.5.cloned.1.call-start = ((), (), s32[]{:S(2)}) async-start(), calls=%async_computation.3 | async-start | bytes 7962624 | tf_op jit(solution)/shard_map/all_gather | solution.py:20
  7.9 80.0 %copy-start.2 = (bf16[128,1152]{1,0:T(8,128)(2,1)S(1)}, bf16[128,1152]{1,0:T(8,128)(2,1)}, u32[]{:S(2)}) copy-start(bf16[128,1152]{1,0:T(8,128)(2,1)} %param.8) | copy-start | bytes 884740
  7.9 150.8 %all-gather.3.cloned.1.call-start = ((), (), s32[]{:S(2)}) async-start(), calls=%async_computation.2 | async-start | bytes 7962624 | tf_op jit(solution)/shard_map/all_gather | solution.py:21
  19.5 166.2 %all-to-all-start = ((bf16[128,2,1152]{2,0,1:T(8,128)(2,1)}), bf16[128,2,1152]{2,0,1:T(8,128)(2,1)S(1)}, u32[]{:S(2)}, u32[]{:S(2)}) async-start(bf16[128,2,1152]{2,0,1:T(8,128)(2,1)} %copy.13), calls=%async_computation | async-start | bytes 1179648 | tf_op jit(solution)/shard_map/all_to_all | solution.py:51
  23.0 199.1 %reduce-scatter.4.cloned.1.call-start = ((), (), s32[]{:S(2)}) async-start(), calls=%async_computation.4 | async-start | bytes 626688 | tf_op jit(solution)/shard_map/reduce_scatter | solution.py:35
  87.9 74.8 %slice-start = ((s8[5308416]{0:T(1024)(128)(4,1)}), s8[1114112]{0:T(1024)(128)(4,1)S(1)}, s32[]{:S(2)}) async-start(s8[5308416]{0:T(1024)(128)(4,1)} %bitcast.30), calls=%async_computation.5 | async-start | bytes 2228224
  158.7 4.0 %slice-start.1 = ((s8[5308416]{0:T(1024)(128)(4,1)}), s8[4194304]{0:T(1024)(128)(4,1)S(1)}, s32[]{:S(2)}) async-start(s8[5308416]{0:T(1024)(128)(4,1)} %bitcast.30), calls=%async_computation.6 | async-start | bytes 8388608
  162.7 2.5 copy-start.1
  212.7 4.7 %copy-start = (f32[1152,1152]{1,0:T(8,128)S(1)}, f32[1152,1152]{1,0:T(8,128)}, u32[]{:S(2)}) copy-start(f32[1152,1152]{1,0:T(8,128)} %get-tuple-element.114) | copy-start | bytes 15925252
Sparse Core Ops, SparseCore 0:
  9.5 78.3 all-gather.4
  89.4 69.2 all-gather.2
  168.0 54.0 reduce-scatter.3
where the time goes:
time: 267 us; the launch traced here: 266 us
  waiting for transfers between devices  135 us (51%)
  blocking collectives  61.8 us (23%)
  other arithmetic  27.3 us (10%)
  matrix products  21.2 us (8%)
  between operations  13.9 us (5%)
  starting transfers between devices  3.64 us (1%)
  local copies, waits for them, and re-layouts  3.38 us (1%)
    all_gather x1, waiting for transfers between devices, shards(): lax.all_gather(w_up, 'dp', axis=0, tiled=True)  67.1 us
    all_gather x1, waiting for transfers between devices, shards(): lax.all_gather(w_gate, 'dp', axis=0, tiled=True)  63.6 us
    psum x1, blocking collectives, shards(): row_sum = lax.psum(row_part, ('tp', 'section'))  29.5 us
    add x2, other arithmetic, one_block(): total + lax.optimization_barrier(term.astype(jnp.bfloat16)).astype(jnp.fl...  16.6 us
    all_gather x1, blocking collectives, shards(): piece_up = lax.all_gather(d_up, 'dp', axis=0, tiled=True)  9.34 us
    all_gather x1, blocking collectives, shards(): rows_in = lax.all_gather(tokens, 'section', axis=1, tiled=True)  9.03 us
    all_gather x1, blocking collectives, shards(): piece_gate = lax.all_gather(d_gate, 'dp', axis=0, tiled=True)  8.47 us
    dot_general x2, matrix products, one_block(): lax.dot_general(block_normed, block_gate, contract_rows, preferred_elemen...  6.71 us
  transfers between devices with their start and end apart: 4, of which 3 were waited for; matrix products, arithmetic and copies ran while one was open for 18% of the time, Pallas kernels for 0%

commit v1 on v0

--- a/solution.py
+++ b/solution.py
@@ -42,7 +42,7 @@
     gain_part = jnp.sum(d_normed * own_inputs * inv_rms[:, None], axis=0)
     row_part = jnp.sum(own_inputs * own_gain * d_normed, axis=1)
     grad_gain = lax.psum(gain_part, "dp")
-    row_sum = lax.psum(row_part, ("tp", "section"))
+    row_sum = jnp.sum(lax.all_gather(row_part, ("tp", "section")), axis=0)
     grad_tokens = (
         inv_rms[:, None] * own_gain * d_normed - own_inputs * (inv_rms**3 * row_sum / D)[:, None]
     )

time: 267 us -> 257 us (0.963)
  blocking collectives: 61.8 us -> 51.7 us
    psum x1 -> x0, blocking collectives: 29.5 us -> none  [shards(): row_sum = lax.psum(row_part, ('tp', 'section'))]
    all_gather x0 -> x1, blocking collectives: none -> 19.4 us  [shards(): row_sum = jnp.sum(lax.all_gather(row_part, ('tp', 'section')), axis=0)]
  transfers between devices with their start and end apart: 4 -> 4, of which waited for: 3 -> 3; matrix products, arithmetic and copies ran while one was open for 18% -> 19% of each run, Pallas kernels for 0% -> 0%
where the time goes in v1:
time: 257 us; the launch traced here: 256 us
  waiting for transfers between devices  135 us (53%)
  blocking collectives  51.7 us (20%)
  other arithmetic  27.3 us (11%)
  matrix products  21.2 us (8%)
  between operations  13.9 us (5%)
  starting transfers between devices  3.64 us (1%)
  local copies, waits for them, and re-layouts  3.38 us (1%)
    all_gather x1, waiting for transfers between devices, shards(): lax.all_gather(w_up, 'dp', axis=0, tiled=True)  67.1 us
    all_gather x1, waiting for transfers between devices, shards(): lax.all_gather(w_gate, 'dp', axis=0, tiled=True)  63.6 us
    all_gather x1, blocking collectives, shards(): row_sum = jnp.sum(lax.all_gather(row_part, ('tp', 'section')), axis=0)  19.4 us
    add x2, other arithmetic, one_block(): total + lax.optimization_barrier(term.astype(jnp.bfloat16)).astype(jnp.fl...  16.6 us
    all_gather x1, blocking collectives, shards(): piece_up = lax.all_gather(d_up, 'dp', axis=0, tiled=True)  9.34 us
    all_gather x1, blocking collectives, shards(): rows_in = lax.all_gather(tokens, 'section', axis=1, tiled=True)  9.03 us
    all_gather x1, blocking collectives, shards(): piece_gate = lax.all_gather(d_gate, 'dp', axis=0, tiled=True)  8.47 us
    dot_general x2, matrix products, one_block(): lax.dot_general(block_normed, block_gate, contract_rows, preferred_elemen...  6.71 us
  transfers between devices with their start and end apart: 4, of which 3 were waited for; matrix products, arithmetic and copies ran while one was open for 19% of the time, Pallas kernels for 0%

profile of v1, /device:TPU:0, one launch (start us, length us, event | category | flops | bytes accessed | tf_op | source)
XLA Modules:
  0.0 256.2 jit_solution(18416864660479428824)
XLA Ops:
  8.7 9.0 %all_gather.21 = bf16[128,2304]{0,1:T(8,128)(2,1)S(1)} all-gather(bf16[128,576]{0,1:T(8,128)(2,1)S(1)} %copy-done.3), channel_id=1, replica_groups=mesh['dp'=2,'tp'=4,'section'=4] {'section'}, dimensions={1}, use_global_device_ids=true | all-gather | bytes 737280 | tf_op jit(solution)/shard_map/all_gather | solution.py:15
  19.5 3.5 %all-to-all-start = ((bf16[128,2,1152]{2,0,1:T(8,128)(2,1)}), bf16[128,2,1152]{2,0,1:T(8,128)(2,1)S(1)}, u32[]{:S(2)}, u32[]{:S(2)}) async-start(bf16[128,2,1152]{2,0,1:T(8,128)(2,1)} %copy.13), calls=%async_computation | async-start | bytes 1179648 | tf_op jit(solution)/shard_map/all_to_all | solution.py:51
  23.1 1.1 convert_element_type.59
  24.3 63.6 %all-gather.7.cloned.1.call-done = bf16[2304,1152]{1,0:T(8,128)(2,1)} async-done(((bf16[1152,1152]{1,0:T(8,128)(2,1)}), bf16[2304,1152]{1,0:T(8,128)(2,1)}) %all-gather.7.cloned.1.call-update) | async-done | bytes 5308432 | tf_op jit(solution)/shard_map/all_gather | solution.py:20
  87.9 3.7 %fusion.8 = (bf16[128,1152]{1,0:T(8,128)(2,1)S(1)}, f32[128,1152]{1,0:T(8,128)S(1)}) fusion(bf16[128,1152]{1,0:T(8,128)(2,1)S(1)} %copy-done.2, bf16[128,2304]{0,1:T(8,128)(2,1)S(1)} %multiply_convert_fusion, bf16[2304,1152]{1,0:T(8,128)(2,1)} %all-gather.7.cloned.1.call-done), kind=kOutput, calls=%fused_computation.19 | convolution fusion | flops 681099264 | bytes 7077888 | tf_op jit(solution)/shard_map/dot_general | solution.py:23
  91.6 67.1 %all-gather.5.cloned.1.call-done = bf16[2304,1152]{1,0:T(8,128)(2,1)} async-done(((bf16[1152,1152]{1,0:T(8,128)(2,1)}), bf16[2304,1152]{1,0:T(8,128)(2,1)}) %all-gather.5.cloned.1.call-update) | async-done | bytes 5308432 | tf_op jit(solution)/shard_map/all_gather | solution.py:21
  158.7 4.0 %fusion.15 = bf16[128,1152]{1,0:T(8,128)(2,1)S(1)} fusion(f32[128,1152]{1,0:T(8,128)S(1)} %get-tuple-element.158, bf16[128,2304]{0,1:T(8,128)(2,1)S(1)} %multiply_convert_fusion, bf16[2304,1152]{1,0:T(8,128)(2,1)} %all-gather.5.cloned.1.call-done, bf16[128,1152]{1,0:T(8,128)(2,1)} %param.8), kind=kOutput, calls=%fused_computation.26 | convolution fusion | flops 682721280 | bytes 7077888 | tf_op jit(solution)/shard_map/dot_general | solution.py:24
  162.7 1.6 fusion.23
  165.2 1.6 fusion.7
  167.9 9.3 %all_gather.27 = bf16[256,1152]{1,0:T(8,128)(2,1)} all-gather(bf16[128,1152]{1,0:T(8,128)(2,1)S(1)} %get-tuple-element.157), channel_id=1, replica_groups=mesh['dp'=2,'tp'=4,'section'=4] {'dp'}, dimensions={0}, use_global_device_ids=true | all-gather | bytes 884736 | tf_op jit(solution)/shard_map/all_gather | solution.py:55
  177.2 8.5 %all_gather.26 = bf16[256,1152]{1,0:T(8,128)(2,1)} all-gather(bf16[128,1152]{1,0:T(8,128)(2,1)S(1)} %fusion.15), channel_id=1, replica_groups=mesh['dp'=2,'tp'=4,'section'=4] {'dp'}, dimensions={0}, use_global_device_ids=true | all-gather | bytes 884736 | tf_op jit(solution)/shard_map/all_gather | solution.py:54
  185.7 27.0 %while.16 = (s32[]{:T(128)}, f32[1152,1152]{1,0:T(8,128)}, f32[1152,1152]{1,0:T(8,128)}, bf16[256,1152]{1,0:T(8,128)(2,1)S(1)}, bf16[256,1152]{1,0:T(8,128)(2,1)...) while((s32[]{:T(128)}, f32[1152,1152]{1,0:T(8,128)}, ...), condition=%wide.region_7.0_spmd.clone, body=%wide.region_6.0_spmd.clone.sunk | while | flops 690094080 | bytes 33032356 | solution.py:77
  185.7 1.8 convolution_convert_fusion.4
  187.6 3.4 %convolution_convert_fusion.5 = bf16[1152,1152]{1,0:T(8,128)(2,1)} fusion(bf16[256,1152]{1,0:T(8,128)(2,1)} %get-tuple-element.224, s32[]{:T(128)S(6)} %select_n.16, bf16[256,1152]{1,0:T(8,128)(2,1)S(1)} %get-tuple-element.223), kind=kOutput, calls=%fused_computation.1.clone.1 | convolution fusion | flops 341065728 | bytes 3245056 | tf_op jit(solution)/shard_map/while/body/eval_jaxpr/dot_general | solution.py:63
  190.9 6.7 %select_add_fusion.3 = (f32[1152,1152]{1,0:T(8,128)}, f32[1152,1152]{1,0:T(8,128)}) fusion(f32[1152,1152]{1,0:T(8,128)} %get-tuple-element.212, bf16[1152,1152]{1,0:T(8,128)(2,1)S(1)} %convolution_convert_fusion.4, pred[]{:T(512)S(6)} %compare.3, bf16[1152,1152]{1,0:T(8,128)(2,1)} %convolution_convert_fusion.5, f32[1152,1152]{1,0:T(8,128)} %get-tuple-element.211), kind=kLoop, calls=%fused_computation.2.clone.1 | loop fusion | flops 7962624 | bytes 26542080 | tf_op jit(solution)/shard_map/while/body/eval_jaxpr/add | solution.py:72
  197.6 1.8 convolution_convert_fusion.4
  199.5 3.4 %convolution_convert_fusion.5 = bf16[1152,1152]{1,0:T(8,128)(2,1)} fusion(bf16[256,1152]{1,0:T(8,128)(2,1)} %get-tuple-element.224, s32[]{:T(128)S(6)} %select_n.16, bf16[256,1152]{1,0:T(8,128)(2,1)S(1)} %get-tuple-element.223), kind=kOutput, calls=%fused_computation.1.clone.1 | convolution fusion | flops 341065728 | bytes 3245056 | tf_op jit(solution)/shard_map/while/body/eval_jaxpr/dot_general | solution.py:63
  202.8 9.9 %select_add_fusion.3 = (f32[1152,1152]{1,0:T(8,128)}, f32[1152,1152]{1,0:T(8,128)}) fusion(f32[1152,1152]{1,0:T(8,128)} %get-tuple-element.212, bf16[1152,1152]{1,0:T(8,128)(2,1)S(1)} %convolution_convert_fusion.4, pred[]{:T(512)S(6)} %compare.3, bf16[1152,1152]{1,0:T(8,128)(2,1)} %convolution_convert_fusion.5, f32[1152,1152]{1,0:T(8,128)} %get-tuple-element.211), kind=kLoop, calls=%fused_computation.2.clone.1 | loop fusion | flops 7962624 | bytes 26542080 | tf_op jit(solution)/shard_map/while/body/eval_jaxpr/add | solution.py:72
  212.7 4.4 %convert_element_type.68 = bf16[1152,1152]{1,0:T(8,128)(2,1)} convert(f32[1152,1152]{1,0:T(8,128)} %get-tuple-element.115) | non-fusion elementwise | flops 1327104 | bytes 7962624 | tf_op jit(solution)/shard_map/convert_element_type | solution.py:84
  217.3 1.8 convert_element_type.67
  219.1 3.0 %reduce-scatter.4.cloned.1.call-done = bf16[144,128]{1,0:T(8,128)(2,1)} async-done(((bf16[2304,128]{1,0:T(8,128)(2,1)}), bf16[144,128]{1,0:T(8,128)(2,1)}) %reduce-scatter.4.cloned.1.call-update) | async-done | bytes 36880 | tf_op jit(solution)/shard_map/reduce_scatter | solution.py:35
  223.2 5.5 %psum.7 = f32[144]{0:T(256)} all-reduce(f32[144]{0:T(256)S(1)} %get-tuple-element.141), channel_id=1, replica_groups=mesh['dp'=2,'tp'=4,'section'=4] {'dp'}, use_global_device_ids=true, to_apply=%region_5.0 | all-reduce | flops 144 | bytes 1152 | tf_op jit(solution)/shard_map/psum | solution.py:44
  228.6 19.4 %all-gather.1 = f32[16,1,128]{2,1,0:T(1,128)S(1)} all-gather(f32[1,1,128]{2,1,0:T(1,128)S(1)} %bitcast.34), channel_id=2, replica_groups=mesh['dp'=2,'tp'=4,'section'=4] {'tp','section'}, dimensions={0}, use_global_device_ids=true | all-gather | bytes 8704 | tf_op jit(solution)/shard_map/all_gather | solution.py:45
  248.1 1.6 fusion.17
  (33 shorter events, 6.7 us)
Async XLA Ops:
  7.2 1.5 copy-start.3
  7.2 10.9 %copy-start.4 = (f32[2304]{0:T(1024)S(1)}, f32[2304]{0:T(1024)}, u32[]{:S(2)}) copy-start(f32[2304]{0:T(1024)} %param.9) | copy-start | bytes 27652
  7.2 80.7 %all-gather.7.cloned.1.call-start = ((), (), s32[]{:S(2)}) async-start(), calls=%async_computation.3 | async-start | bytes 7962624 | tf_op jit(solution)/shard_map/all_gather | solution.py:20
  7.9 80.0 %copy-start.2 = (bf16[128,1152]{1,0:T(8,128)(2,1)S(1)}, bf16[128,1152]{1,0:T(8,128)(2,1)}, u32[]{:S(2)}) copy-start(bf16[128,1152]{1,0:T(8,128)(2,1)} %param.8) | copy-start | bytes 884740
  7.9 150.8 %all-gather.5.cloned.1.call-start = ((), (), s32[]{:S(2)}) async-start(), calls=%async_computation.2 | async-start | bytes 7962624 | tf_op jit(solution)/shard_map/all_gather | solution.py:21
  19.5 166.2 %all-to-all-start = ((bf16[128,2,1152]{2,0,1:T(8,128)(2,1)}), bf16[128,2,1152]{2,0,1:T(8,128)(2,1)S(1)}, u32[]{:S(2)}, u32[]{:S(2)}) async-start(bf16[128,2,1152]{2,0,1:T(8,128)(2,1)} %copy.13), calls=%async_computation | async-start | bytes 1179648 | tf_op jit(solution)/shard_map/all_to_all | solution.py:51
  23.0 199.1 %reduce-scatter.4.cloned.1.call-start = ((), (), s32[]{:S(2)}) async-start(), calls=%async_computation.4 | async-start | bytes 626688 | tf_op jit(solution)/shard_map/reduce_scatter | solution.py:35
  87.9 74.8 %slice-start = ((s8[5308416]{0:T(1024)(128)(4,1)}), s8[1114112]{0:T(1024)(128)(4,1)S(1)}, s32[]{:S(2)}) async-start(s8[5308416]{0:T(1024)(128)(4,1)} %bitcast.31), calls=%async_computation.5 | async-start | bytes 2228224
  158.7 4.0 %slice-start.1 = ((s8[5308416]{0:T(1024)(128)(4,1)}), s8[4194304]{0:T(1024)(128)(4,1)S(1)}, s32[]{:S(2)}) async-start(s8[5308416]{0:T(1024)(128)(4,1)} %bitcast.31), calls=%async_computation.6 | async-start | bytes 8388608
  162.7 2.5 copy-start.1
  212.7 4.7 %copy-start = (f32[1152,1152]{1,0:T(8,128)S(1)}, f32[1152,1152]{1,0:T(8,128)}, u32[]{:S(2)}) copy-start(f32[1152,1152]{1,0:T(8,128)} %get-tuple-element.114) | copy-start | bytes 15925252
Sparse Core Ops, SparseCore 0:
  9.5 78.3 all-gather.6
  89.4 69.2 all-gather.4
  168.0 54.0 reduce-scatter.3
